TPU v7x, 32 devices: a whole 2x2x4 slice. The times are simulated.
32 devices in a mesh: dp: 32 (over z, y, x, core).
Axes of the slice: x: 2, y: 2, z: 4, core: 2. Of those that a mesh axis runs over, the one named last changes fastest.
Arguments:
- attended: bfloat16 [16384, 1152], P('dp'), may hold values from -24 to 24, as said below
- proj_cot: bfloat16 [16384, 1152], P('dp'), may hold values from -0.0007324219 to 0.0007324219
- timesteps: float32 [64], P('dp'), may hold values from 0 to 1
- embed_cot: bfloat16 [64, 1152], P('dp'), may hold values from -0.03125 to 0.03125
- master_proj: float32 [1327104], P('dp'), may hold values from -0.1875 to 0.1875
- moment_proj: float32 [1327104], P('dp'), may hold values from -0.013671875 to 0.013671875
- second_proj: float32 [1327104], P('dp'), may hold values from 1.8838011e-07 to 3.0140818e-06
- master_embed: float32 [294912], P('dp'), may hold values from -0.375 to 0.375
- moment_embed: float32 [294912], P('dp'), may hold values from -0.02734375 to 0.02734375
- squared_moment_layer: float32 [294912], P('dp'), may hold values from 8.477105e-07 to 1.3563368e-05
- attended_next: bfloat16 [16384, 1152], P('dp'), may hold values from -6 to 6
- timesteps_next: float32 [64], P('dp'), may hold values from 0 to 1
Outputs:
- next_proj: bfloat16 [16384, 1152], P('dp')
- next_embed: bfloat16 [64, 1152], P('dp')
- move_direction_output: float32 [1327104], P('dp')
- step_embed: float32 [294912], P('dp')
- master_proj_new: float32 [1327104], P('dp')
- master_embed_new: float32 [294912], P('dp')
- grad_norm: float32 [], replicated
Inputs may be any that keep to these rules, and one draw needn't show every extreme that they name: attended has entries of mean zero whose scale differs between feature columns by up to a factor of 16.
All inputs are finite; a program needn't handle non-finite values.
Results may differ from a plain program's by a relative error of at most 0.0025.
Values may be sent and summed in bfloat16 or wider, within the bound.
A program may use at most 64 MiB of HBM per device.

v0:
```python
import math

import jax
import jax.numpy as jnp
from jax import lax
from jax.sharding import PartitionSpec as P

beta_one = 0.9
beta_two = 0.999
step_count = 1000.0
learn_rate = 0.0001
shrink_factor = 0.01
epsilon = 1e-08
max_norm = 1.0


def freq_embed(moments, width):
    half_width = width // 2
    ladder = jnp.arange(half_width, dtype=jnp.float32)
    freqs = jnp.exp(-math.log(10000.0) * ladder / half_width)
    phase_values = (moments * 1000.0)[:, None] * freqs[None, :]
    return jnp.concatenate([jnp.cos(phase_values), jnp.sin(phase_values)], axis=1).astype(
        jnp.bfloat16
    )


def adamw_update(gradient, clip, master, moment, second):
    scaled = clip * gradient
    first_new = beta_one * moment + (1.0 - beta_one) * scaled
    second_new = beta_two * second + (1.0 - beta_two) * scaled * scaled
    first_hat = first_new / (1.0 - beta_one**step_count)
    second_hat = second_new / (1.0 - beta_two**step_count)
    direction = first_hat / (jnp.sqrt(second_hat) + epsilon)
    freshened_values = master - learn_rate * (direction + shrink_factor * master)
    return (direction, freshened_values)


def per_device(
    attended,
    proj_cot,
    timesteps,
    embed_cot,
    master_proj,
    moment_proj,
    second_proj,
    master_embed,
    moment_embed,
    squared_moment_layer,
    attended_next,
    timesteps_next,
):
    width = attended.shape[1]
    freq_width = master_embed.shape[0] * lax.axis_size("dp") // width
    term_proj = jnp.dot(attended.T, proj_cot, preferred_element_type=jnp.float32).reshape(-1)
    freq_now = freq_embed(timesteps, freq_width)
    term_embed = jnp.dot(freq_now.T, embed_cot, preferred_element_type=jnp.float32).reshape(-1)
    grad_proj, grad_embed = (
        lax.psum_scatter(term_proj, "dp", scatter_dimension=0, tiled=True),
        lax.psum_scatter(term_embed, "dp", scatter_dimension=0, tiled=True),
    )
    square_proj = lax.psum(jnp.sum(grad_proj * grad_proj), "dp")
    square_embed = lax.psum(jnp.sum(grad_embed * grad_embed), "dp")
    total = square_proj + square_embed
    grad_norm = jnp.sqrt(total)
    clip = jnp.minimum(jnp.float32(1.0), max_norm / (grad_norm + 1e-06))
    move_direction_output, master_proj_new = adamw_update(
        grad_proj, clip, master_proj, moment_proj, second_proj
    )
    step_embed, master_embed_new = adamw_update(
        grad_embed, clip, master_embed, moment_embed, squared_moment_layer
    )
    shard_proj = master_proj_new.astype(jnp.bfloat16)
    shard_embed = master_embed_new.astype(jnp.bfloat16)
    whole_proj = lax.all_gather(shard_proj, "dp", axis=0, tiled=True)
    whole_embed = lax.all_gather(shard_embed, "dp", axis=0, tiled=True)
    weight_proj = whole_proj.reshape(width, width)
    weight_embed = whole_embed.reshape(freq_width, width)
    next_proj = jnp.dot(attended_next, weight_proj, preferred_element_type=jnp.float32).astype(
        jnp.bfloat16
    )
    freq_next = freq_embed(timesteps_next, freq_width)
    next_embed = jnp.dot(freq_next, weight_embed, preferred_element_type=jnp.float32).astype(
        jnp.bfloat16
    )
    return (
        next_proj,
        next_embed,
        move_direction_output,
        step_embed,
        master_proj_new,
        master_embed_new,
        grad_norm,
    )


def solution(mesh):
    in_specs = (
        P("dp", None),
        P("dp", None),
        P("dp"),
        P("dp", None),
        P("dp"),
        P("dp"),
        P("dp"),
        P("dp"),
        P("dp"),
        P("dp"),
        P("dp", None),
        P("dp"),
    )
    out_specs = (P("dp", None), P("dp", None), P("dp"), P("dp"), P("dp"), P("dp"), P())
    return jax.shard_map(
        per_device, mesh=mesh, in_specs=in_specs, out_specs=out_specs, check_vma=False
    )
```

profile of v0, /device:TPU:1, one launch (start us, length us, event | category | flops | bytes accessed | tf_op | source)
XLA Modules:
  0.0 365.2 jit_solution(16386064144316177083)
XLA Ops:
  7.2 0.0 copy-start
  7.2 0.0 all-reduce.5.cloned.1.call-start
  7.2 0.8 broadcast_multiply_fusion
  8.0 0.1 fusion.13
  8.1 1.1 fusion.15
  9.2 0.0 copy-start.1
  9.2 1.1 reshape.34
  10.3 0.0 copy-done
  10.3 0.6 copy-done.1
  10.9 4.1 %fusion.28 = f32[1152,1152]{1,0:T(8,128)} fusion(bf16[512,1152]{1,0:T(8,128)(2,1)S(1)} %copy-done, bf16[512,1152]{1,0:T(8,128)(2,1)S(1)} %copy-done.1), kind=kOutput, calls=%fused_computation.41 | convolution fusion | flops 1358954496 | bytes 7667712 | tf_op jit(solution)/shard_map/dot_general | solution.py:54
  15.0 6.5 %reshape.33 = f32[1327104]{0:T(1024)} reshape(f32[1152,1152]{1,0:T(8,128)} %fusion.28) | data formatting | bytes 10616832 | tf_op jit(solution)/shard_map/reshape | solution.py:54
  21.5 0.0 copy-start.2
  21.5 0.0 copy-start.3
  21.5 0.0 copy-start.4
  21.5 0.0 all-reduce.5.cloned.1.call-update
  21.5 0.0 copy-start.5
  21.6 0.0 copy-start.6
  21.6 0.0 copy-start.7
  21.6 0.0 all-gather.3.cloned.1.call-start
  21.6 160.8 %all-reduce.5.cloned.1.call-done = (f32[1327104]{0:T(1024)}, f32[294912]{0:T(1024)}) async-done(((f32[1327104]{0:T(1024)}, f32[294912]{0:T(1024)}), (f32[1327104]{0:T(1024)}, f32[294912]{0:T(1024)})) %all-reduce.5.cloned.1.call-update) | async-done | bytes 6488080
  182.4 1.6 multiply_reduce_fusion
  184.1 1.4 multiply_reduce_fusion.1
  186.7 39.3 %psum.16 = f32[]{:T(128)} all-reduce(f32[]{:T(128)S(6)} %add.44), channel_id=1, replica_groups=mesh['dp'=32] {'dp'}, use_global_device_ids=true, to_apply=%region_2.0 | all-reduce | flops 1 | bytes 8 | tf_op jit(solution)/shard_map/psum | solution.py:61
  226.8 0.0 copy-done.2
  226.8 0.0 copy-done.3
  226.8 0.0 copy-done.4
  226.8 1.9 fusion.26
  228.7 0.8 reshape.37
  229.4 0.0 all-gather.3.cloned.1.call-update
  229.5 0.0 copy-done.5
  229.5 0.0 copy-done.6
  229.5 0.0 copy-done.7
  229.5 1.4 fusion.24
  230.9 44.3 %all_gather.7 = bf16[294912]{0:T(1024)(128)(2,1)S(1)} all-gather(bf16[9216]{0:T(1024)(128)(2,1)S(1)} %get-tuple-element.30), channel_id=1, replica_groups=mesh['dp'=32] {'dp'}, dimensions={0}, use_global_device_ids=true | all-gather | bytes 608256 | tf_op jit(solution)/shard_map/all_gather | solution.py:75
  275.3 0.7 reshape.36
  276.0 0.8 convolution_convert_fusion.1
  276.8 20.5 %all-gather.3.cloned.1.call-done = bf16[32,1,41472]{2,1,0:T(2,128)(2,1)} async-done(((bf16[1,1,41472]{2,1,0:T(2,128)(2,1)}), bf16[32,1,41472]{2,1,0:T(2,128)(2,1)}) %all-gather.3.cloned.1.call-update) | async-done | bytes 2654224 | tf_op jit(solution)/shard_map/all_gather | solution.py:74
  297.3 48.6 %reduce = bf16[32,41472]{1,0:T(8,128)(2,1)} reduce(bf16[32,1,41472]{2,1,0:T(2,128)(2,1)} %all-gather.3.cloned.1.call-done, bf16[]{:T(256)} %constant.50), dimensions={1}, to_apply=%all-gather.reduce_sub_computation | reduce | bytes 5308418 | tf_op jit(solution)/shard_map/all_gather | solution.py:74
  345.9 0.0 copy-start.8
  345.9 6.5 %reshape.35 = bf16[1152,1152]{1,0:T(8,128)(2,1)} reshape(bf16[32,41472]{1,0:T(8,128)(2,1)} %reduce) | data formatting | bytes 5308416 | tf_op jit(solution)/shard_map/reshape | solution.py:76
  352.4 0.0 copy-done.8
  352.4 3.5 fusion
  355.9 1.4 copy.21
  (1 shorter events, 0.0 us)
Async XLA Ops:
  7.2 3.1 copy-start
  7.2 175.2 %all-reduce.5.cloned.1.call-start = ((), (), s32[]{:S(2)}) async-start(), calls=%async_computation.1 | async-start | bytes 12976128
  9.2 1.7 copy-start.1
  21.5 205.3 %copy-start.2 = (f32[41472]{0:T(1024)S(1)}, f32[41472]{0:T(1024)}, u32[]{:S(2)}) copy-start(f32[41472]{0:T(1024)} %param.16) | copy-start | bytes 497668
  21.5 205.3 %copy-start.3 = (f32[41472]{0:T(1024)S(1)}, f32[41472]{0:T(1024)}, u32[]{:S(2)}) copy-start(f32[41472]{0:T(1024)} %param.18) | copy-start | bytes 497668
  21.5 205.3 %copy-start.4 = (f32[41472]{0:T(1024)S(1)}, f32[41472]{0:T(1024)}, u32[]{:S(2)}) copy-start(f32[41472]{0:T(1024)} %param.17) | copy-start | bytes 497668
  21.5 207.9 %copy-start.5 = (f32[9216]{0:T(1024)S(1)}, f32[9216]{0:T(1024)}, u32[]{:S(2)}) copy-start(f32[9216]{0:T(1024)} %param.19) | copy-start | bytes 110596
  21.6 207.9 %copy-start.6 = (f32[9216]{0:T(1024)S(1)}, f32[9216]{0:T(1024)}, u32[]{:S(2)}) copy-start(f32[9216]{0:T(1024)} %param.21) | copy-start | bytes 110596
  21.6 207.9 %copy-start.7 = (f32[9216]{0:T(1024)S(1)}, f32[9216]{0:T(1024)}, u32[]{:S(2)}) copy-start(f32[9216]{0:T(1024)} %param.20) | copy-start | bytes 110596
  21.6 275.7 %all-gather.3.cloned.1.call-start = ((), (), s32[]{:S(2)}) async-start(), calls=%async_computation | async-start | bytes 5474304 | tf_op jit(solution)/shard_map/all_gather | solution.py:74
  345.9 6.5 %copy-start.8 = (bf16[512,1152]{1,0:T(8,128)(2,1)S(1)}, bf16[512,1152]{1,0:T(8,128)(2,1)}, u32[]{:S(2)}) copy-start(bf16[512,1152]{1,0:T(8,128)(2,1)} %param.22) | copy-start | bytes 3538948
Sparse Core Ops, SparseCore 0:
  21.7 160.7 all-reduce.4
  229.6 67.6 all-gather.2
where the time goes:
time: 366 us; the launch traced here: 365 us
  waiting for transfers between devices  181 us (49%)
  blocking collectives  83.7 us (23%)
  other arithmetic  55.8 us (15%)
  local copies, waits for them, and re-layouts  17.6 us (5%)
  between operations  17.3 us (5%)
  matrix products  9.43 us (3%)
    unnamed x3, waiting for transfers between devices  161 us
    all_gather x1, other arithmetic, per_device(): whole_proj = lax.all_gather(shard_proj, 'dp', axis=0, tiled=True)  48.6 us
    all_gather x1, blocking collectives, per_device(): whole_embed = lax.all_gather(shard_embed, 'dp', axis=0, tiled=True)  44.3 us
    psum x1, blocking collectives, per_device(): square_proj = lax.psum(jnp.sum(grad_proj * grad_proj), 'dp')  39.3 us
    all_gather x1, waiting for transfers between devices, per_device(): whole_proj = lax.all_gather(shard_proj, 'dp', axis=0, tiled=True)  20.5 us
  transfers between devices with their start and end apart: 2, of which 2 were waited for; matrix products, arithmetic and copies ran while one was open for 1% of the time, Pallas kernels for 0%

commit v1 on v0

v1 whole, which is shorter than its diff:
```python
import functools
import math

import jax
import jax.numpy as jnp
from jax import lax
from jax.experimental import pallas as pl
from jax.experimental.pallas import tpu as pltpu
from jax.sharding import PartitionSpec as P

beta_one = 0.9
beta_two = 0.999
step_count = 1000.0
learn_rate = 0.0001
shrink_factor = 0.01
epsilon = 1e-08
max_norm = 1.0


def freq_embed(moments, width):
    half_width = width // 2
    ladder = jnp.arange(half_width, dtype=jnp.float32)
    freqs = jnp.exp(-math.log(10000.0) * ladder / half_width)
    phase_values = (moments * 1000.0)[:, None] * freqs[None, :]
    return jnp.concatenate([jnp.cos(phase_values), jnp.sin(phase_values)], axis=1).astype(
        jnp.bfloat16
    )


def adamw_update(gradient, clip, master, moment, second):
    scaled = clip * gradient
    first_new = beta_one * moment + (1.0 - beta_one) * scaled
    second_new = beta_two * second + (1.0 - beta_two) * scaled * scaled
    first_hat = first_new / (1.0 - beta_one**step_count)
    second_hat = second_new / (1.0 - beta_two**step_count)
    direction = first_hat / (jnp.sqrt(second_hat) + epsilon)
    freshened_values = master - learn_rate * (direction + shrink_factor * master)
    return (direction, freshened_values)


LANES = 128
MESH = pl.DeviceIdType.MESH


def round_up(value, step):
    return -(-value // step) * step


def factor(n):
    bits = (n // 2).bit_length() - 1
    z_bits = -(-bits // 3)
    y_bits = -(-(bits - z_bits) // 2)
    return 2**z_bits, 2**y_bits, 2 ** (bits - z_bits - y_bits)


def exchange_kernel(
    n,
    rows,
    rows_embed,
    grad_p,
    grad_e,
    master_p,
    moment_p,
    second_p,
    master_e,
    moment_e,
    second_e,
    weight_p,
    weight_e,
    step_p,
    step_e,
    new_p,
    new_e,
    norm_out,
    stage,
    mine,
    g,
    r0,
    a1,
    r_a,
    a2,
    r_b,
    a3,
    r_z,
    norm_src,
    norm_all,
    w,
    c_sem,
    a_sem,
    b_sem,
    z_sem,
    n_sem,
    gz_sem,
    gb_sem,
    ga_sem,
    gc_sem,
):
    nz, ny, nx = factor(n)
    q = nx
    columns = grad_p.shape[1] // LANES
    flat_e = rows_embed * columns
    flat_p = rows * columns
    base_p = round_up(flat_e, 8)
    depth = g.shape[-2]
    group = stage.shape[0] // depth

    me = lax.axis_index("dp")
    c = lax.rem(me, 2)
    x = lax.rem(me // 2, nx)
    y = lax.rem(me // (2 * nx), ny)
    z = me // (2 * nx * ny)
    first = c == 0
    a, b = jnp.where(first, x, y), jnp.where(first, y, x)
    stride_a, stride_b = jnp.where(first, 2, 2 * nx), jnp.where(first, 2 * nx, 2)

    def device(z_at, a_at, b_at):
        return z_at * (2 * nx * ny) + a_at * stride_a + b_at * stride_b + c

    partner = me + 1 - 2 * c

    def place(d):
        core = lax.rem(d, 2)
        dx = lax.rem(d // 2, nx)
        dy = lax.rem(d // (2 * nx), ny)
        return (
            core,
            d // (2 * nx * ny),
            jnp.where(core == 0, dx, dy),
            jnp.where(core == 0, dy, dx),
        )

    def remote(src, dst, sems, at, target):
        return pltpu.make_async_remote_copy(
            src_ref=src,
            dst_ref=dst,
            send_sem=sems.at[(0, *at)],
            recv_sem=sems.at[(1, *at)],
            device_id=(target,),
            device_id_type=MESH,
        )

    barrier = pltpu.get_barrier_semaphore()

    @pl.loop(1, n)
    def _(r):
        pl.semaphore_signal(
            barrier, inc=1, device_id=(lax.rem(me + r, n),), device_id_type=MESH
        )

    stage[...] = jnp.zeros_like(stage)

    @pl.loop(0, n // group)
    def _(p):
        top_p = pl.multiple_of(p * (group * rows), 16)
        top_e = pl.multiple_of(p * (group * rows_embed), 16)
        for j in range(columns):
            lanes = slice(j * LANES, (j + 1) * LANES)
            values_p = grad_p[pl.ds(top_p, group * rows), lanes]
            values_e = grad_e[pl.ds(top_e, group * rows_embed), lanes]
            for i in range(group):
                stage[pl.ds(i * depth + base_p + j, rows, stride=columns), :] = values_p[
                    i * rows : (i + 1) * rows
                ]
                stage[pl.ds(i * depth + j, rows_embed, stride=columns), :] = values_e[
                    i * rows_embed : (i + 1) * rows_embed
                ]
        for i in range(group):
            core, dz, da, db = place(p * group + i)
            g[core, dz, da, db] = stage[i * depth : (i + 1) * depth].astype(g.dtype)

    pl.semaphore_wait(barrier, n - 1)

    order = [lax.rem(z + 1 + k, nz) for k in range(nz)]
    c_copies, a_copies, b_copies, z_copies = [], [], [], []
    for k, zk in enumerate(order):
        copy = remote(g.at[1 - c, zk], r0.at[zk], c_sem, (k,), partner)
        copy.start()
        c_copies.append(copy)
    for k, zk in enumerate(order):
        c_copies[k].wait_recv()
        for i in range(q):
            for j in range(q):
                a1[zk, i, j] = (
                    g[c, zk, i, j].astype(jnp.float32) + r0[zk, i, j].astype(jnp.float32)
                ).astype(a1.dtype)
        for s in range(1, q):
            to = lax.rem(a + s, q)
            copy = remote(
                a1.at[zk, to], r_a.at[s - 1, zk], a_sem, (s - 1, k), device(z, to, b)
            )
            copy.start()
            a_copies.append(copy)
    for k, zk in enumerate(order):
        for s in range(1, q):
            a_copies[k * (q - 1) + s - 1].wait_recv()
        for j in range(q):
            total = a1[zk, a, j].astype(jnp.float32)
            for s in range(1, q):
                total = total + r_a[s - 1, zk, j].astype(jnp.float32)
            a2[zk, j] = total.astype(a2.dtype)
        for s in range(1, q):
            to = lax.rem(b + s, q)
            copy = remote(
                a2.at[zk, to], r_b.at[s - 1, zk], b_sem, (s - 1, k), device(z, a, to)
            )
            copy.start()
            b_copies.append(copy)
    for k, zk in enumerate(order):
        for s in range(1, q):
            b_copies[k * (q - 1) + s - 1].wait_recv()
        total = a2[zk, b].astype(jnp.float32)
        for s in range(1, q):
            total = total + r_b[s - 1, zk].astype(jnp.float32)
        if k < nz - 1:
            a3[k] = total.astype(a3.dtype)
            copy = remote(a3.at[k], r_z.at[k], z_sem, (k,), device(zk, a, b))
            copy.start()
            z_copies.append(copy)
        else:
            mine[...] = total
    for copy in z_copies:
        copy.wait_recv()
    total = mine[...]
    for k in range(nz - 1):
        total = total + r_z[k].astype(jnp.float32)
    mine[...] = total

    norm_src[...] = jnp.sum(total * total, axis=0, keepdims=True)
    norm_all[me] = norm_src[...]

    @pl.loop(1, n)
    def _(r):
        remote(norm_src, norm_all.at[me], n_sem, (), lax.rem(me + r, n)).start()

    others = norm_all.at[pl.ds(0, n - 1)]
    norm_copies = remote(others, others, n_sem, (), partner)
    norm_copies.wait_recv()
    norm = jnp.sqrt(jnp.sum(jnp.sum(norm_all[...], axis=0), axis=1, keepdims=True))
    clip = jnp.minimum(jnp.float32(1.0), max_norm / (norm + 1e-06))
    norm_out[...] = jnp.broadcast_to(norm, norm_out.shape)

    step, new = adamw_update(
        mine[base_p : base_p + flat_p], clip, master_p[...], moment_p[...], second_p[...]
    )
    step_p[...] = step
    new_p[...] = new
    stage[base_p : base_p + flat_p] = new
    step, new = adamw_update(mine[:flat_e], clip, master_e[...], moment_e[...], second_e[...])
    step_e[...] = step
    new_e[...] = new
    stage[:flat_e] = new
    w[c, z, a, b] = stage[:depth].astype(w.dtype)

    sent = []

    def forward(block, z_at, sems, at, target):
        copy = remote(block, block, sems, at, target)
        copy.start()
        sent.append(copy)

    def back(index, by, size):
        return lax.rem(index + size - by, size)

    own = w.at[c, z, a, b]
    for k in range(nz - 1):
        forward(own, z, gz_sem, (k,), device(order[k], a, b))
    for t in range(nz):
        z_t = back(z, t, nz)
        block = w.at[c, z_t, a, b]
        if t:
            remote(block, block, gz_sem, (t - 1,), partner).wait_recv()
        for s in range(1, q):
            forward(block, z_t, ga_sem, (s - 1, t, 0), device(z, lax.rem(a + s, q), b))
        for s in range(1, q):
            forward(block, z_t, gb_sem, (s - 1, t), device(z, a, lax.rem(b + s, q)))
        forward(block, z_t, gc_sem, (t, 0, 0), partner)
    for t in range(nz):
        z_t = back(z, t, nz)
        for kb in range(1, q):
            block = w.at[c, z_t, a, back(b, kb, q)]
            remote(block, block, gb_sem, (kb - 1, t), partner).wait_recv()
            for s in range(1, q):
                forward(block, z_t, ga_sem, (s - 1, t, kb), device(z, lax.rem(a + s, q), b))
            forward(block, z_t, gc_sem, (t, kb, 0), partner)
    for t in range(nz):
        z_t = back(z, t, nz)
        for kb in range(q):
            for ka in range(1, q):
                block = w.at[c, z_t, back(a, ka, q), back(b, kb, q)]
                remote(block, block, ga_sem, (ka - 1, t, kb), partner).wait_recv()
                forward(block, z_t, gc_sem, (t, kb, ka), partner)
    for t in range(nz):
        for kb in range(q):
            for ka in range(q):
                block = w.at[1 - c, back(z, t, nz), back(b, ka, q), back(a, kb, q)]
                remote(block, block, gc_sem, (t, kb, ka), partner).wait_recv()

    @pl.loop(0, n // group)
    def _(p):
        top_p = pl.multiple_of(p * (group * rows), 16)
        top_e = pl.multiple_of(p * (group * rows_embed), 16)
        for i in range(group):
            core, dz, da, db = place(p * group + i)
            stage[i * depth : (i + 1) * depth] = w[core, dz, da, db].astype(jnp.float32)
        for j in range(columns):
            lanes = slice(j * LANES, (j + 1) * LANES)
            weight_p[pl.ds(top_p, group * rows), lanes] = jnp.concatenate(
                [
                    stage[pl.ds(i * depth + base_p + j, rows, stride=columns), :]
                    for i in range(group)
                ],
                axis=0,
            ).astype(weight_p.dtype)
            weight_e[pl.ds(top_e, group * rows_embed), lanes] = jnp.concatenate(
                [
                    stage[pl.ds(i * depth + j, rows_embed, stride=columns), :]
                    for i in range(group)
                ],
                axis=0,
            ).astype(weight_e.dtype)

    for copy in c_copies + a_copies + b_copies + z_copies + sent:
        copy.wait_send()
    norm_copies.wait_send()


def exchange(n, grad_p, grad_e, states):
    nz, ny, nx = factor(n)
    width = grad_p.shape[1]
    columns = width // LANES
    rows, rows_embed = grad_p.shape[0] // n, grad_e.shape[0] // n
    group = max(16 // math.gcd(rows, 16), 16 // math.gcd(rows_embed, 16))
    depth = round_up(round_up(rows_embed * columns, 8) + rows * columns, 16)
    f32, bf16 = jnp.float32, jnp.bfloat16
    q = nx
    assert nx == ny and n % group == 0

    def dma(*sizes):
        return pltpu.SemaphoreType.DMA((2, *(max(size, 1) for size in sizes)))

    flat_p = jax.ShapeDtypeStruct((rows * columns, LANES), f32)
    flat_e = jax.ShapeDtypeStruct((rows_embed * columns, LANES), f32)
    vmem = pl.BlockSpec(memory_space=pltpu.VMEM)
    return pl.pallas_call(
        functools.partial(exchange_kernel, n, rows, rows_embed),
        out_shape=(
            jax.ShapeDtypeStruct(grad_p.shape, bf16),
            jax.ShapeDtypeStruct(grad_e.shape, bf16),
            flat_p,
            flat_e,
            flat_p,
            flat_e,
            jax.ShapeDtypeStruct((1, LANES), f32),
        ),
        in_specs=[vmem] * 8,
        out_specs=(vmem,) * 7,
        scratch_shapes=[
            pltpu.VMEM((group * depth, LANES), f32),
            pltpu.VMEM((depth, LANES), f32),
            pltpu.VMEM((2, nz, q, q, depth, LANES), bf16),
            pltpu.VMEM((nz, q, q, depth, LANES), bf16),
            pltpu.VMEM((nz, q, q, depth, LANES), bf16),
            pltpu.VMEM((q - 1, nz, q, depth, LANES), bf16),
            pltpu.VMEM((nz, q, depth, LANES), bf16),
            pltpu.VMEM((q - 1, nz, depth, LANES), bf16),
            pltpu.VMEM((nz - 1, depth, LANES), bf16),
            pltpu.VMEM((nz - 1, depth, LANES), bf16),
            pltpu.VMEM((1, LANES), f32),
            pltpu.VMEM((n, 1, LANES), f32),
            pltpu.VMEM((2, nz, q, q, depth, LANES), bf16),
            dma(nz),
            dma(q - 1, nz),
            dma(q - 1, nz),
            dma(nz - 1),
            dma(),
            dma(nz - 1),
            dma(q - 1, nz),
            dma(q - 1, nz, q),
            dma(nz, q, q),
        ],
        compiler_params=pltpu.CompilerParams(
            collective_id=0, has_side_effects=True, vmem_limit_bytes=56 * 2**20
        ),
    )(grad_p, grad_e, *(state.reshape(-1, LANES) for state in states))


def per_device(
    attended,
    proj_cot,
    timesteps,
    embed_cot,
    master_proj,
    moment_proj,
    second_proj,
    master_embed,
    moment_embed,
    squared_moment_layer,
    attended_next,
    timesteps_next,
):
    width = attended.shape[1]
    freq_width = master_embed.shape[0] * lax.axis_size("dp") // width
    n = lax.axis_size("dp")
    grad_proj = jnp.dot(attended.T, proj_cot, preferred_element_type=jnp.float32)
    freq_now = freq_embed(timesteps, freq_width)
    grad_embed = jnp.dot(freq_now.T, embed_cot, preferred_element_type=jnp.float32)
    states = (
        master_proj,
        moment_proj,
        second_proj,
        master_embed,
        moment_embed,
        squared_moment_layer,
    )
    weight_proj, weight_embed, step_p, step_e, new_p, new_e, norm = exchange(
        n, grad_proj, grad_embed, states
    )
    next_proj = jnp.dot(attended_next, weight_proj, preferred_element_type=jnp.float32).astype(
        jnp.bfloat16
    )
    freq_next = freq_embed(timesteps_next, freq_width)
    next_embed = jnp.dot(freq_next, weight_embed, preferred_element_type=jnp.float32).astype(
        jnp.bfloat16
    )
    return (
        next_proj,
        next_embed,
        step_p.reshape(-1),
        step_e.reshape(-1),
        new_p.reshape(-1),
        new_e.reshape(-1),
        norm[0, 0],
    )


def solution(mesh):
    in_specs = (
        P("dp", None),
        P("dp", None),
        P("dp"),
        P("dp", None),
        P("dp"),
        P("dp"),
        P("dp"),
        P("dp"),
        P("dp"),
        P("dp"),
        P("dp", None),
        P("dp"),
    )
    out_specs = (P("dp", None), P("dp", None), P("dp"), P("dp"), P("dp"), P("dp"), P())
    return jax.shard_map(
        per_device, mesh=mesh, in_specs=in_specs, out_specs=out_specs, check_vma=False
    )
```

time: 366 us -> 81.7 us (0.22)
  waiting for transfers between devices: 181 us -> 0 us
  blocking collectives: 83.7 us -> 0 us
  Pallas kernels: 0 us -> 64.1 us
  other arithmetic: 55.8 us -> 0.96 us
  between operations: 17.3 us -> 1.89 us
  local copies, waits for them, and re-layouts: 17.6 us -> 4.05 us
    unnamed x3 -> x0, waiting for transfers between devices: 161 us -> none
    pallas_call x0 -> x1, Pallas kernels: none -> 64.1 us  [exchange(): pl.pallas_call(functools.partial(exchange_kernel, n, rows, rows_embed), o...]
    all_gather x1 -> x0, other arithmetic: 48.6 us -> none  [per_device(): whole_proj = lax.all_gather(shard_proj, 'dp', axis=0, tiled=True)]
    all_gather x1 -> x0, blocking collectives: 44.3 us -> none  [per_device(): whole_embed = lax.all_gather(shard_embed, 'dp', axis=0, tiled=True)]
    psum x1 -> x0, blocking collectives: 39.3 us -> none  [per_device(): square_proj = lax.psum(jnp.sum(grad_proj * grad_proj), 'dp')]
    all_gather x1 -> x0, waiting for transfers between devices: 20.5 us -> none  [per_device(): whole_proj = lax.all_gather(shard_proj, 'dp', axis=0, tiled=True)]
    reshape x4 -> x0, local copies, waits for them, and re-layouts: 14.8 us -> none  [the longest x1 6.54 us: per_device(): jnp.dot(attended.T, proj_cot, preferred_element_type=jnp.float32)]
  transfers between devices with their start and end apart: 2 -> 0, of which waited for: 2 -> 0; matrix products, arithmetic and copies ran while one was open for 1% -> 0% of each run, Pallas kernels for 0% -> 0%
where the time goes in v1:
time: 81.7 us; the launch traced here: 81.4 us
  Pallas kernels  64.1 us (78%)
  matrix products  10.4 us (13%)
  local copies, waits for them, and re-layouts  4.05 us (5%)
  between operations  1.89 us (2%)
  other arithmetic  0.96 us (1%)
    pallas_call x1, Pallas kernels, exchange(): pl.pallas_call(functools.partial(exchange_kernel, n, rows, rows_embed), o...  64.1 us
    dot_general x1, matrix products, per_device(): jnp.dot(attended.T, proj_cot, preferred_element_type=jnp.float32)  4.06 us
    unnamed x23, local copies, waits for them, and re-layouts  4.05 us
    dot_general x1, matrix products, per_device(): jnp.dot(attended_next, weight_proj, preferred_element_type=jnp.float32)  3.5 us
    dot_general x1, matrix products, per_device(): jnp.dot(freq_now.T, embed_cot, preferred_element_type=jnp.float32)  2.07 us

profile of v1, /device:TPU:1, one launch (start us, length us, event | category | flops | bytes accessed | tf_op | source)
XLA Modules:
  0.0 81.4 jit_solution(1828047915362883363)
XLA Ops:
  0.6 0.0 copy-start
  0.6 0.0 copy-start.1
  0.7 0.8 %broadcast_multiply_fusion = (f32[2]{0:T(128)S(1)}, f32[2]{0:T(128)S(1)}) fusion(f32[2]{0:T(128)} %param.23, f32[2]{0:T(128)} %param.14), kind=kLoop, calls=%fused_computation.19 | loop fusion | flops 4 | bytes 32 | tf_op jit(solution)/shard_map/mul | solution.py:24
  1.5 0.1 fusion.3
  1.6 2.1 %fusion.5.grad_e = f32[256,1152]{1,0:T(8,128)} fusion(bf16[2,1152]{1,0:T(2,128)(2,1)} %param.15, bf16[2,128]{1,0:T(2,128)(2,1)S(1)} %get-tuple-element.32, bf16[2,128]{1,0:T(2,128)(2,1)S(1)} %get-tuple-element.33), kind=kOutput, calls=%fused_computation.11 | convolution fusion | flops 1181696 | bytes 1185280 | tf_op jit(solution)/shard_map/dot_general | solution.py:406
  3.7 0.0 copy-done
  3.7 0.0 copy-done.1
  3.7 4.1 %fusion.14.grad_p = f32[1152,1152]{1,0:T(8,128)} fusion(bf16[512,1152]{1,0:T(8,128)(2,1)S(1)} %copy-done, bf16[512,1152]{1,0:T(8,128)(2,1)S(1)} %copy-done.1), kind=kOutput, calls=%fused_computation.23 | convolution fusion | flops 1358954496 | bytes 7667712 | tf_op jit(solution)/shard_map/dot_general | solution.py:404
  7.8 0.0 copy-start.7
  7.8 64.1 %shard_map.171 = (bf16[1152,1152]{1,0:T(8,128)(2,1)}, bf16[256,1152]{1,0:T(8,128)(2,1)}, f32[324,128]{1,0:T(8,128)}, f32[72,128]{1,0:T(8,128)}, f32[324,128]{1,0...) custom-call(f32[1152,1152]{1,0:T(8,128)} %fusion.14.grad_p, f32[256,1152]{1,0:T(8,128)} %fusion.5.grad_e, ...), custom_call_target="tpu_custom_call" | custom-call | tf_op jit(solution)/shard_map/pallas_call | solution.py:344
  71.8 0.0 copy-done.7
  71.9 3.5 %fusion = bf16[512,1152]{0,1:T(8,128)(2,1)S(1)} fusion(bf16[1152,1152]{1,0:T(8,128)(2,1)} %get-tuple-element.14, bf16[512,1152]{1,0:T(8,128)(2,1)S(1)} %copy-done.7), kind=kOutput, calls=%fused_computation.1 | convolution fusion | flops 1359544320 | bytes 5013504 | tf_op jit(solution)/shard_map/dot_general | solution.py:418
  75.4 0.0 copy-start.2
  75.4 0.0 copy-start.4
  75.4 0.0 copy-start.6
  75.4 0.0 copy-start.3
  75.4 1.4 %copy.19 = bf16[512,1152]{1,0:T(8,128)(2,1)} copy(bf16[512,1152]{0,1:T(8,128)(2,1)S(1)} %fusion) | data formatting | bytes 2359296
  76.8 0.0 copy-done.2
  76.8 0.0 copy-start.5
  76.8 0.0 copy-start.8
  76.8 0.8 convolution_convert_fusion.1
  77.6 0.0 copy-done.4
  77.6 0.7 copy.25
  78.3 0.0 copy-done.6
  78.3 0.6 copy.26
  78.9 0.0 copy-done.3
  78.9 0.7 copy.27
  79.6 0.0 copy-done.5
  79.6 0.6 copy.28
  80.2 0.0 copy-done.8
  (1 shorter events, 0.0 us)
Async XLA Ops:
  0.6 3.1 %copy-start = (bf16[512,1152]{1,0:T(8,128)(2,1)S(1)}, bf16[512,1152]{1,0:T(8,128)(2,1)}, u32[]{:S(2)}) copy-start(bf16[512,1152]{1,0:T(8,128)(2,1)} %param.12) | copy-start | bytes 3538948
  0.6 3.0 %copy-start.1 = (bf16[512,1152]{1,0:T(8,128)(2,1)S(1)}, bf16[512,1152]{1,0:T(8,128)(2,1)}, u32[]{:S(2)}) copy-start(bf16[512,1152]{1,0:T(8,128)(2,1)} %param.13) | copy-start | bytes 3538948
  7.8 64.1 %copy-start.7 = (bf16[512,1152]{1,0:T(8,128)(2,1)S(1)}, bf16[512,1152]{1,0:T(8,128)(2,1)}, u32[]{:S(2)}) copy-start(bf16[512,1152]{1,0:T(8,128)(2,1)} %param.22) | copy-start | bytes 3538948
  75.4 1.5 %copy-start.2 = (bf16[256,1152]{1,0:T(8,128)(2,1)S(1)}, bf16[256,1152]{1,0:T(8,128)(2,1)}, u32[]{:S(2)}) copy-start(bf16[256,1152]{1,0:T(8,128)(2,1)} %get-tuple-element.15) | copy-start | bytes 1769476
  75.4 2.2 %copy-start.4 = (f32[324,128]{1,0:T(8,128)S(1)}, f32[324,128]{1,0:T(8,128)}, u32[]{:S(2)}) copy-start(f32[324,128]{1,0:T(8,128)} %get-tuple-element.16) | copy-start | bytes 497668
  75.4 2.9 %copy-start.6 = (f32[72,128]{1,0:T(8,128)S(1)}, f32[72,128]{1,0:T(8,128)}, u32[]{:S(2)}) copy-start(f32[72,128]{1,0:T(8,128)} %get-tuple-element.17) | copy-start | bytes 110596
  75.4 3.5 %copy-start.3 = (f32[324,128]{1,0:T(8,128)S(1)}, f32[324,128]{1,0:T(8,128)}, u32[]{:S(2)}) copy-start(f32[324,128]{1,0:T(8,128)} %get-tuple-element.18) | copy-start | bytes 497668
  76.8 2.8 %copy-start.5 = (f32[72,128]{1,0:T(8,128)S(1)}, f32[72,128]{1,0:T(8,128)}, u32[]{:S(2)}) copy-start(f32[72,128]{1,0:T(8,128)} %get-tuple-element.19) | copy-start | bytes 110596
  76.8 3.4 %copy-start.8 = (f32[1,128]{1,0:T(1,128)S(1)}, f32[1,128]{1,0:T(1,128)}, u32[]{:S(2)}) copy-start(f32[1,128]{1,0:T(1,128)} %get-tuple-element.20) | copy-start | bytes 1540

commit v2 on v1

--- a/solution.py
+++ b/solution.py
@@ -57,21 +57,29 @@
     n,
     rows,
     rows_embed,
-    grad_p,
-    grad_e,
+    attended,
+    proj_cot,
+    freq_now,
+    embed_cot,
+    attended_next,
+    freq_next,
     master_p,
     moment_p,
     second_p,
     master_e,
     moment_e,
     second_e,
-    weight_p,
-    weight_e,
+    next_p,
+    next_e,
     step_p,
     step_e,
     new_p,
     new_e,
     norm_out,
+    grad_p,
+    grad_e,
+    weight_p,
+    weight_e,
     stage,
     mine,
     g,
@@ -147,65 +155,84 @@
             barrier, inc=1, device_id=(lax.rem(me + r, n),), device_id_type=MESH
         )
 
+    span = block_of(attended.shape[1])
+
+    @pl.loop(0, attended.shape[1] // span)
+    def _(i):
+        top = pl.multiple_of(i * span, span)
+        grad_p[pl.ds(top, span), :] = lax.dot_general(
+            attended[:, pl.ds(top, span)],
+            proj_cot[...],
+            (((0,), (0,)), ((), ())),
+            preferred_element_type=jnp.float32,
+        )
+
+    total = None
+    for i in range(embed_cot.shape[0]):
+        term = freq_now[:, i : i + 1] * embed_cot[i : i + 1, :].astype(jnp.float32)
+        total = term if total is None else total + term
+    grad_e[...] = total
+
     stage[...] = jnp.zeros_like(stage)
-
-    @pl.loop(0, n // group)
-    def _(p):
-        top_p = pl.multiple_of(p * (group * rows), 16)
-        top_e = pl.multiple_of(p * (group * rows_embed), 16)
-        for j in range(columns):
-            lanes = slice(j * LANES, (j + 1) * LANES)
-            values_p = grad_p[pl.ds(top_p, group * rows), lanes]
-            values_e = grad_e[pl.ds(top_e, group * rows_embed), lanes]
+    order = [lax.rem(z + 1 + k, nz) for k in range(nz)]
+    groups = n // group // nz
+    c_copies, a_copies, b_copies, z_copies = [], [], [], []
+
+    def flatten(zk):
+        @pl.loop(zk * groups, zk * groups + groups)
+        def _(p):
+            top_p = pl.multiple_of(p * (group * rows), 16)
+            top_e = pl.multiple_of(p * (group * rows_embed), 16)
+            for j in range(columns):
+                lanes = slice(j * LANES, (j + 1) * LANES)
+                values_p = grad_p[pl.ds(top_p, group * rows), lanes]
+                values_e = grad_e[pl.ds(top_e, group * rows_embed), lanes]
+                for i in range(group):
+                    stage[pl.ds(i * depth + base_p + j, rows, stride=columns), :] = values_p[
+                        i * rows : (i + 1) * rows
+                    ]
+                    stage[pl.ds(i * depth + j, rows_embed, stride=columns), :] = values_e[
+                        i * rows_embed : (i + 1) * rows_embed
+                    ]
             for i in range(group):
-                stage[pl.ds(i * depth + base_p + j, rows, stride=columns), :] = values_p[
-                    i * rows : (i + 1) * rows
-                ]
-                stage[pl.ds(i * depth + j, rows_embed, stride=columns), :] = values_e[
-                    i * rows_embed : (i + 1) * rows_embed
-                ]
-        for i in range(group):
-            core, dz, da, db = place(p * group + i)
-            g[core, dz, da, db] = stage[i * depth : (i + 1) * depth].astype(g.dtype)
-
-    pl.semaphore_wait(barrier, n - 1)
-
-    order = [lax.rem(z + 1 + k, nz) for k in range(nz)]
-    c_copies, a_copies, b_copies, z_copies = [], [], [], []
-    for k, zk in enumerate(order):
-        copy = remote(g.at[1 - c, zk], r0.at[zk], c_sem, (k,), partner)
-        copy.start()
-        c_copies.append(copy)
-    for k, zk in enumerate(order):
+                core, dz, da, db = place(p * group + i)
+                g[core, dz, da, db] = stage[i * depth : (i + 1) * depth].astype(g.dtype)
+
+    def reduce_core(k):
+        zk = order[k]
         c_copies[k].wait_recv()
-        for i in range(q):
+        for s in range(1, q + 1):
+            i = lax.rem(a + s, q)
             for j in range(q):
                 a1[zk, i, j] = (
                     g[c, zk, i, j].astype(jnp.float32) + r0[zk, i, j].astype(jnp.float32)
                 ).astype(a1.dtype)
-        for s in range(1, q):
-            to = lax.rem(a + s, q)
-            copy = remote(
-                a1.at[zk, to], r_a.at[s - 1, zk], a_sem, (s - 1, k), device(z, to, b)
-            )
-            copy.start()
-            a_copies.append(copy)
-    for k, zk in enumerate(order):
+            if s < q:
+                copy = remote(
+                    a1.at[zk, i], r_a.at[s - 1, zk], a_sem, (s - 1, k), device(z, i, b)
+                )
+                copy.start()
+                a_copies.append(copy)
+
+    def reduce_a(k):
+        zk = order[k]
         for s in range(1, q):
             a_copies[k * (q - 1) + s - 1].wait_recv()
-        for j in range(q):
+        for s in range(1, q + 1):
+            j = lax.rem(b + s, q)
             total = a1[zk, a, j].astype(jnp.float32)
-            for s in range(1, q):
-                total = total + r_a[s - 1, zk, j].astype(jnp.float32)
+            for r in range(1, q):
+                total = total + r_a[r - 1, zk, j].astype(jnp.float32)
             a2[zk, j] = total.astype(a2.dtype)
-        for s in range(1, q):
-            to = lax.rem(b + s, q)
-            copy = remote(
-                a2.at[zk, to], r_b.at[s - 1, zk], b_sem, (s - 1, k), device(z, a, to)
-            )
-            copy.start()
-            b_copies.append(copy)
-    for k, zk in enumerate(order):
+            if s < q:
+                copy = remote(
+                    a2.at[zk, j], r_b.at[s - 1, zk], b_sem, (s - 1, k), device(z, a, j)
+                )
+                copy.start()
+                b_copies.append(copy)
+
+    def reduce_b(k):
+        zk = order[k]
         for s in range(1, q):
             b_copies[k * (q - 1) + s - 1].wait_recv()
         total = a2[zk, b].astype(jnp.float32)
@@ -218,6 +245,21 @@
             z_copies.append(copy)
         else:
             mine[...] = total
+
+    for k in range(nz + 3):
+        if k < nz:
+            flatten(order[k])
+            if k == 0:
+                pl.semaphore_wait(barrier, n - 1)
+            copy = remote(g.at[1 - c, order[k]], r0.at[order[k]], c_sem, (k,), partner)
+            copy.start()
+            c_copies.append(copy)
+        if 0 <= k - 1 < nz:
+            reduce_core(k - 1)
+        if 0 <= k - 2 < nz:
+            reduce_a(k - 2)
+        if 0 <= k - 3 < nz:
+            reduce_b(k - 3)
     for copy in z_copies:
         copy.wait_recv()
     total = mine[...]
@@ -264,17 +306,19 @@
     own = w.at[c, z, a, b]
     for k in range(nz - 1):
         forward(own, z, gz_sem, (k,), device(order[k], a, b))
-    for t in range(nz):
+
+    def gather_z(t):
         z_t = back(z, t, nz)
         block = w.at[c, z_t, a, b]
         if t:
             remote(block, block, gz_sem, (t - 1,), partner).wait_recv()
         for s in range(1, q):
+            forward(block, z_t, gb_sem, (s - 1, t), device(z, a, lax.rem(b + s, q)))
+        for s in range(1, q):
             forward(block, z_t, ga_sem, (s - 1, t, 0), device(z, lax.rem(a + s, q), b))
-        for s in range(1, q):
-            forward(block, z_t, gb_sem, (s - 1, t), device(z, a, lax.rem(b + s, q)))
         forward(block, z_t, gc_sem, (t, 0, 0), partner)
-    for t in range(nz):
+
+    def gather_b(t):
         z_t = back(z, t, nz)
         for kb in range(1, q):
             block = w.at[c, z_t, a, back(b, kb, q)]
@@ -282,58 +326,93 @@
             for s in range(1, q):
                 forward(block, z_t, ga_sem, (s - 1, t, kb), device(z, lax.rem(a + s, q), b))
             forward(block, z_t, gc_sem, (t, kb, 0), partner)
-    for t in range(nz):
+
+    def gather_a(t):
         z_t = back(z, t, nz)
         for kb in range(q):
             for ka in range(1, q):
                 block = w.at[c, z_t, back(a, ka, q), back(b, kb, q)]
                 remote(block, block, ga_sem, (ka - 1, t, kb), partner).wait_recv()
                 forward(block, z_t, gc_sem, (t, kb, ka), partner)
-    for t in range(nz):
+
+    def unflatten(t):
+        z_t = back(z, t, nz)
         for kb in range(q):
             for ka in range(q):
-                block = w.at[1 - c, back(z, t, nz), back(b, ka, q), back(a, kb, q)]
+                block = w.at[1 - c, z_t, back(b, ka, q), back(a, kb, q)]
                 remote(block, block, gc_sem, (t, kb, ka), partner).wait_recv()
 
-    @pl.loop(0, n // group)
-    def _(p):
-        top_p = pl.multiple_of(p * (group * rows), 16)
-        top_e = pl.multiple_of(p * (group * rows_embed), 16)
-        for i in range(group):
-            core, dz, da, db = place(p * group + i)
-            stage[i * depth : (i + 1) * depth] = w[core, dz, da, db].astype(jnp.float32)
-        for j in range(columns):
-            lanes = slice(j * LANES, (j + 1) * LANES)
-            weight_p[pl.ds(top_p, group * rows), lanes] = jnp.concatenate(
-                [
-                    stage[pl.ds(i * depth + base_p + j, rows, stride=columns), :]
-                    for i in range(group)
-                ],
-                axis=0,
-            ).astype(weight_p.dtype)
-            weight_e[pl.ds(top_e, group * rows_embed), lanes] = jnp.concatenate(
-                [
-                    stage[pl.ds(i * depth + j, rows_embed, stride=columns), :]
-                    for i in range(group)
-                ],
-                axis=0,
-            ).astype(weight_e.dtype)
+        @pl.loop(z_t * groups, z_t * groups + groups)
+        def _(p):
+            top_p = pl.multiple_of(p * (group * rows), 16)
+            top_e = pl.multiple_of(p * (group * rows_embed), 16)
+            for i in range(group):
+                core, dz, da, db = place(p * group + i)
+                stage[i * depth : (i + 1) * depth] = w[core, dz, da, db].astype(jnp.float32)
+            for j in range(columns):
+                lanes = slice(j * LANES, (j + 1) * LANES)
+                weight_p[pl.ds(top_p, group * rows), lanes] = jnp.concatenate(
+                    [
+                        stage[pl.ds(i * depth + base_p + j, rows, stride=columns), :]
+                        for i in range(group)
+                    ],
+                    axis=0,
+                ).astype(weight_p.dtype)
+                weight_e[pl.ds(top_e, group * rows_embed), lanes] = jnp.concatenate(
+                    [
+                        stage[pl.ds(i * depth + j, rows_embed, stride=columns), :]
+                        for i in range(group)
+                    ],
+                    axis=0,
+                ).astype(weight_e.dtype)
+
+    for t in range(nz + 3):
+        if t < nz:
+            gather_z(t)
+        if 0 <= t - 1 < nz:
+            gather_b(t - 1)
+        if 0 <= t - 2 < nz:
+            gather_a(t - 2)
+        if 0 <= t - 3 < nz:
+            unflatten(t - 3)
+
+    next_e[...] = jnp.dot(
+        freq_next[...], weight_e[...], preferred_element_type=jnp.float32
+    ).astype(next_e.dtype)
+
+    @pl.loop(0, weight_p.shape[1] // span)
+    def _(i):
+        left = pl.multiple_of(i * span, span)
+        next_p[:, pl.ds(left, span)] = jnp.dot(
+            attended_next[...], weight_p[:, pl.ds(left, span)], preferred_element_type=jnp.float32
+        ).astype(next_p.dtype)
 
     for copy in c_copies + a_copies + b_copies + z_copies + sent:
         copy.wait_send()
     norm_copies.wait_send()
 
 
-def exchange(n, grad_p, grad_e, states):
+def block_of(width):
+    return next(size for size in (384, 256, 128) if width % size == 0)
+
+
+def copy_kernel(*refs):
+    half = len(refs) // 2
+    for source, result in zip(refs[:half], refs[half:]):
+        result[...] = source[...]
+
+
+def exchange(n, attended, proj_cot, freq_now, embed_cot, attended_next, freq_next, states):
     nz, ny, nx = factor(n)
-    width = grad_p.shape[1]
+    width = attended.shape[1]
+    width_e = freq_now.shape[0]
     columns = width // LANES
-    rows, rows_embed = grad_p.shape[0] // n, grad_e.shape[0] // n
+    rows, rows_embed = width // n, width_e // n
     group = max(16 // math.gcd(rows, 16), 16 // math.gcd(rows_embed, 16))
     depth = round_up(round_up(rows_embed * columns, 8) + rows * columns, 16)
     f32, bf16 = jnp.float32, jnp.bfloat16
     q = nx
-    assert nx == ny and n % group == 0
+    assert nx == ny and n % (group * nz) == 0
 
     def dma(*sizes):
         return pltpu.SemaphoreType.DMA((2, *(max(size, 1) for size in sizes)))
@@ -341,20 +420,25 @@
     flat_p = jax.ShapeDtypeStruct((rows * columns, LANES), f32)
     flat_e = jax.ShapeDtypeStruct((rows_embed * columns, LANES), f32)
     vmem = pl.BlockSpec(memory_space=pltpu.VMEM)
-    return pl.pallas_call(
+    results = (
+        jax.ShapeDtypeStruct(attended_next.shape, bf16),
+        jax.ShapeDtypeStruct(embed_cot.shape, bf16),
+        flat_p,
+        flat_e,
+        flat_p,
+        flat_e,
+        jax.ShapeDtypeStruct((1, LANES), f32),
+    )
+    outs = pl.pallas_call(
         functools.partial(exchange_kernel, n, rows, rows_embed),
-        out_shape=(
-            jax.ShapeDtypeStruct(grad_p.shape, bf16),
-            jax.ShapeDtypeStruct(grad_e.shape, bf16),
-            flat_p,
-            flat_e,
-            flat_p,
-            flat_e,
-            jax.ShapeDtypeStruct((1, LANES), f32),
-        ),
-        in_specs=[vmem] * 8,
+        out_shape=results,
+        in_specs=[vmem] * 12,
         out_specs=(vmem,) * 7,
         scratch_shapes=[
+            pltpu.VMEM((width, width), f32),
+            pltpu.VMEM((width_e, width), f32),
+            pltpu.VMEM((width, width), bf16),
+            pltpu.VMEM((width_e, width), bf16),
             pltpu.VMEM((group * depth, LANES), f32),
             pltpu.VMEM((depth, LANES), f32),
             pltpu.VMEM((2, nz, q, q, depth, LANES), bf16),
@@ -379,9 +463,20 @@
             dma(nz, q, q),
         ],
         compiler_params=pltpu.CompilerParams(
-            collective_id=0, has_side_effects=True, vmem_limit_bytes=56 * 2**20
+            collective_id=0, has_side_effects=True, vmem_limit_bytes=44 * 2**20
         ),
-    )(grad_p, grad_e, *(state.reshape(-1, LANES) for state in states))
+    )(
+        attended,
+        proj_cot,
+        freq_now,
+        embed_cot,
+        attended_next,
+        freq_next,
+        *(state.reshape(-1, LANES) for state in states),
+    )
+    return pl.pallas_call(
+        copy_kernel, out_shape=results, in_specs=[vmem] * 7, out_specs=(vmem,) * 7
+    )(*outs)
 
 
 def per_device(
@@ -401,9 +496,8 @@
     width = attended.shape[1]
     freq_width = master_embed.shape[0] * lax.axis_size("dp") // width
     n = lax.axis_size("dp")
-    grad_proj = jnp.dot(attended.T, proj_cot, preferred_element_type=jnp.float32)
-    freq_now = freq_embed(timesteps, freq_width)
-    grad_embed = jnp.dot(freq_now.T, embed_cot, preferred_element_type=jnp.float32)
+    freq_now = freq_embed(timesteps, freq_width).astype(jnp.float32).T
+    freq_next = freq_embed(timesteps_next, freq_width)
     states = (
         master_proj,
         moment_proj,
@@ -412,15 +506,8 @@
         moment_embed,
         squared_moment_layer,
     )
-    weight_proj, weight_embed, step_p, step_e, new_p, new_e, norm = exchange(
-        n, grad_proj, grad_embed, states
-    )
-    next_proj = jnp.dot(attended_next, weight_proj, preferred_element_type=jnp.float32).astype(
-        jnp.bfloat16
-    )
-    freq_next = freq_embed(timesteps_next, freq_width)
-    next_embed = jnp.dot(freq_next, weight_embed, preferred_element_type=jnp.float32).astype(
-        jnp.bfloat16
+    next_proj, next_embed, step_p, step_e, new_p, new_e, norm = exchange(
+        n, attended, proj_cot, freq_now, embed_cot, attended_next, freq_next, states
     )
     return (
         next_proj,

time: 81.7 us -> 77.8 us (0.952)
  matrix products: 10.4 us -> 0 us
  local copies, waits for them, and re-layouts: 4.05 us -> 14.4 us
  Pallas kernels: 64.1 us -> 60.7 us
  between operations: 1.89 us -> 0.7 us
    dot_general x4 -> x0, matrix products: 10.4 us -> none  [the longest x1 4.06 us: per_device(): jnp.dot(attended.T, proj_cot, preferred_element_type=jnp.float32)]
    unnamed x23 -> x34, local copies, waits for them, and re-layouts: 4.05 us -> 14.3 us
    pallas_call x1, Pallas kernels: 64.1 us -> 58.1 us  [exchange(): pl.pallas_call(functools.partial(exchange_kernel, n, rows, rows_embed), o...]
    pallas_call x0 -> x1, Pallas kernels: none -> 2.59 us  [exchange(): pl.pallas_call(copy_kernel, out_shape=results, in_specs=[vmem] * 7, out_s...]
where the time goes in v2:
time: 77.8 us; the launch traced here: 77.3 us
  Pallas kernels  60.7 us (78%)
  local copies, waits for them, and re-layouts  14.4 us (19%)
  other arithmetic  1.45 us (2%)
    pallas_call x1, Pallas kernels, exchange(): pl.pallas_call(functools.partial(exchange_kernel, n, rows, rows_embed), o...  58.1 us
    unnamed x34, local copies, waits for them, and re-layouts  14.3 us
    pallas_call x1, Pallas kernels, exchange(): pl.pallas_call(copy_kernel, out_shape=results, in_specs=[vmem] * 7, out_s...  2.59 us

profile of v2, /device:TPU:1, one launch (start us, length us, event | category | flops | bytes accessed | tf_op | source)
XLA Modules:
  0.0 77.3 jit_solution(1097300722931302585)
XLA Ops:
  0.6 0.7 broadcast_multiply_fusion.1
  1.3 0.7 broadcast_multiply_fusion
  2.0 0.1 fusion.2
  2.1 0.1 copy.19.freq_now
  2.2 0.0 copy-start.1
  2.3 1.3 %copy-done.1 = bf16[512,1152]{1,0:T(8,128)(2,1)S(1)} copy-done((bf16[512,1152]{1,0:T(8,128)(2,1)S(1)}, bf16[512,1152]{1,0:T(8,128)(2,1)}, u32[]{:S(2)}) %copy-start.1) | copy-done | bytes 1179672
  3.5 0.0 copy-start.2
  3.5 1.3 %copy-done.2 = bf16[512,1152]{1,0:T(8,128)(2,1)S(1)} copy-done((bf16[512,1152]{1,0:T(8,128)(2,1)S(1)}, bf16[512,1152]{1,0:T(8,128)(2,1)}, u32[]{:S(2)}) %copy-start.2) | copy-done | bytes 1179672
  4.8 0.0 copy-start.3
  4.8 1.3 %copy-done.3 = bf16[512,1152]{1,0:T(8,128)(2,1)S(1)} copy-done((bf16[512,1152]{1,0:T(8,128)(2,1)S(1)}, bf16[512,1152]{1,0:T(8,128)(2,1)}, u32[]{:S(2)}) %copy-start.3) | copy-done | bytes 1179672
  6.1 0.0 copy-start.6
  6.1 0.9 %copy-done.6 = f32[41472]{0:T(1024)S(1)} copy-done((f32[41472]{0:T(1024)S(1)}, f32[41472]{0:T(1024)}, u32[]{:S(2)}) %copy-start.6) | copy-done | bytes 165912
  7.0 0.0 copy-start.7
  7.0 0.9 %copy-done.7 = f32[41472]{0:T(1024)S(1)} copy-done((f32[41472]{0:T(1024)S(1)}, f32[41472]{0:T(1024)}, u32[]{:S(2)}) %copy-start.7) | copy-done | bytes 165912
  7.9 0.0 copy-start.8
  7.9 0.9 %copy-done.8 = f32[41472]{0:T(1024)S(1)} copy-done((f32[41472]{0:T(1024)S(1)}, f32[41472]{0:T(1024)}, u32[]{:S(2)}) %copy-start.8) | copy-done | bytes 165912
  8.8 0.0 copy-start.11
  8.8 0.8 copy-done.11
  9.6 0.0 copy-start.12
  9.6 0.8 copy-done.12
  10.4 0.0 copy-start.13
  10.4 0.8 copy-done.13
  11.1 0.0 copy-start.14
  11.1 0.7 copy-done.14
  11.8 58.1 %shard_map.171 = (bf16[512,1152]{1,0:T(8,128)(2,1)S(1)}, bf16[2,1152]{1,0:T(2,128)(2,1)S(1)}, f32[324,128]{1,0:T(8,128)S(1)}, f32[72,128]{1,0:T(8,128)S(1)}, f32...) custom-call(bf16[512,1152]{1,0:T(8,128)(2,1)S(1)} %copy-done.1, bf16[512,1152]{1,0:T(8,128)(2,1)S(1)} %copy-done.2, ...), custom_call_target="tpu_custom_call" | custom-call | tf_op jit(solution)/shard_map/pallas_call | solution.py:432
  69.9 0.0 copy-start
  70.0 1.0 %copy-done = bf16[512,1152]{1,0:T(8,128)(2,1)} copy-done((bf16[512,1152]{1,0:T(8,128)(2,1)}, bf16[512,1152]{1,0:T(8,128)(2,1)S(1)}, u32[]{:S(2)}) %copy-start) | copy-done | bytes 1179672
  71.0 0.0 copy-start.4
  71.0 0.7 copy-done.4
  71.6 0.0 copy-start.5
  71.7 0.7 copy-done.5
  72.3 0.0 copy-start.9
  72.3 0.6 copy-done.9
  72.9 0.0 copy-start.10
  72.9 0.6 copy-done.10
  73.5 0.0 copy-start.15
  73.5 0.6 copy-done.15
  74.1 0.0 copy-start.16
  74.1 0.5 copy-done.16
  74.7 2.6 %shard_map.172 = (bf16[512,1152]{1,0:T(8,128)(2,1)}, bf16[2,1152]{1,0:T(2,128)(2,1)}, f32[324,128]{1,0:T(8,128)}, f32[72,128]{1,0:T(8,128)}, f32[324,128]{1,0:T(...) custom-call(bf16[512,1152]{1,0:T(8,128)(2,1)} %copy-done, bf16[2,1152]{1,0:T(2,128)(2,1)} %copy-done.15, ...), custom_call_target="tpu_custom_call" | custom-call | tf_op jit(solution)/shard_map/pallas_call | solution.py:477
  (2 shorter events, 0.0 us)
Async XLA Ops:
  2.2 1.3 %copy-start.1 = (bf16[512,1152]{1,0:T(8,128)(2,1)S(1)}, bf16[512,1152]{1,0:T(8,128)(2,1)}, u32[]{:S(2)}) copy-start(bf16[512,1152]{1,0:T(8,128)(2,1)} %attended.1) | copy-start | bytes 3538948
  3.5 1.3 %copy-start.2 = (bf16[512,1152]{1,0:T(8,128)(2,1)S(1)}, bf16[512,1152]{1,0:T(8,128)(2,1)}, u32[]{:S(2)}) copy-start(bf16[512,1152]{1,0:T(8,128)(2,1)} %proj_cot.1) | copy-start | bytes 3538948
  4.8 1.3 %copy-start.3 = (bf16[512,1152]{1,0:T(8,128)(2,1)S(1)}, bf16[512,1152]{1,0:T(8,128)(2,1)}, u32[]{:S(2)}) copy-start(bf16[512,1152]{1,0:T(8,128)(2,1)} %attended_next.1) | copy-start | bytes 3538948
  6.1 0.9 %copy-start.6 = (f32[41472]{0:T(1024)S(1)}, f32[41472]{0:T(1024)}, u32[]{:S(2)}) copy-start(f32[41472]{0:T(1024)} %param.16) | copy-start | bytes 497668
  7.0 0.9 %copy-start.7 = (f32[41472]{0:T(1024)S(1)}, f32[41472]{0:T(1024)}, u32[]{:S(2)}) copy-start(f32[41472]{0:T(1024)} %param.17) | copy-start | bytes 497668
  7.9 0.9 %copy-start.8 = (f32[41472]{0:T(1024)S(1)}, f32[41472]{0:T(1024)}, u32[]{:S(2)}) copy-start(f32[41472]{0:T(1024)} %param.18) | copy-start | bytes 497668
  8.8 0.8 copy-start.11
  9.6 0.8 copy-start.12
  10.4 0.8 copy-start.13
  11.1 0.7 copy-start.14
  69.9 1.0 %copy-start = (bf16[512,1152]{1,0:T(8,128)(2,1)}, bf16[512,1152]{1,0:T(8,128)(2,1)S(1)}, u32[]{:S(2)}) copy-start(bf16[512,1152]{1,0:T(8,128)(2,1)S(1)} %get-tuple-element.21.refs_0_) | copy-start | bytes 3538948
  71.0 0.7 copy-start.4
  71.6 0.7 copy-start.5
  72.3 0.6 copy-start.9
  72.9 0.6 copy-start.10
  73.5 0.6 copy-start.15
  74.1 0.5 copy-start.16

commit v3 on v2

--- a/solution.py
+++ b/solution.py
@@ -39,6 +39,7 @@
 
 
 LANES = 128
+VMEM_LIMIT = 62 * 2**20
 MESH = pl.DeviceIdType.MESH
 
 
@@ -463,7 +464,7 @@
             dma(nz, q, q),
         ],
         compiler_params=pltpu.CompilerParams(
-            collective_id=0, has_side_effects=True, vmem_limit_bytes=44 * 2**20
+            collective_id=0, has_side_effects=True, vmem_limit_bytes=VMEM_LIMIT
         ),
     )(
         attended,
@@ -475,7 +476,11 @@
         *(state.reshape(-1, LANES) for state in states),
     )
     return pl.pallas_call(
-        copy_kernel, out_shape=results, in_specs=[vmem] * 7, out_specs=(vmem,) * 7
+        copy_kernel,
+        out_shape=results,
+        in_specs=[vmem] * 7,
+        out_specs=(vmem,) * 7,
+        compiler_params=pltpu.CompilerParams(vmem_limit_bytes=VMEM_LIMIT),
     )(*outs)
 
 

time: 77.8 us -> 67.6 us (0.87)
  local copies, waits for them, and re-layouts: 14.4 us -> 0.8 us
  Pallas kernels: 60.7 us -> 63.9 us
    unnamed x34 -> x0, local copies, waits for them, and re-layouts: 14.3 us -> none
    pallas_call x1, Pallas kernels: 58.1 us -> 61.3 us  [exchange(): pl.pallas_call(functools.partial(exchange_kernel, n, rows, rows_embed), o...]
where the time goes in v3:
time: 67.6 us; the launch traced here: 67.4 us
  Pallas kernels  63.9 us (95%)
  other arithmetic  2.01 us (3%)
  local copies, waits for them, and re-layouts  0.8 us (1%)
    pallas_call x1, Pallas kernels, exchange(): pl.pallas_call(functools.partial(exchange_kernel, n, rows, rows_embed), o...  61.3 us
    pallas_call x1, Pallas kernels, exchange(): pl.pallas_call(copy_kernel, out_shape=results, in_specs=[vmem] * 7, out_s...  2.59 us

profile of v3, /device:TPU:1, one launch (start us, length us, event | category | flops | bytes accessed | tf_op | source)
XLA Modules:
  0.0 67.4 jit_solution(4543183837021021928)
XLA Ops:
  0.6 0.7 broadcast_multiply_fusion.1
  1.3 0.7 broadcast_multiply_fusion
  2.0 0.1 fusion.2
  2.1 0.6 convert_bitcast_fusion
  2.7 0.8 %copy.19.freq_now = f32[256,2]{1,0:T(8,128)} copy(f32[256,2]{0,1:T(2,128)S(1)} %get-tuple-element.41) | data formatting | bytes 4096 | tf_op jit(solution)/shard_map/transpose | solution.py:504
  3.5 61.3 %shard_map.171 = (bf16[512,1152]{1,0:T(8,128)(2,1)}, bf16[2,1152]{1,0:T(2,128)(2,1)}, f32[324,128]{1,0:T(8,128)}, f32[72,128]{1,0:T(8,128)}, f32[324,128]{1,0:T(...) custom-call(bf16[512,1152]{1,0:T(8,128)(2,1)} %attended.1, bf16[512,1152]{1,0:T(8,128)(2,1)} %proj_cot.1, ...), custom_call_target="tpu_custom_call" | custom-call | tf_op jit(solution)/shard_map/pallas_call | solution.py:433
  64.8 2.6 %shard_map.172 = (bf16[512,1152]{1,0:T(8,128)(2,1)}, bf16[2,1152]{1,0:T(2,128)(2,1)}, f32[324,128]{1,0:T(8,128)}, f32[72,128]{1,0:T(8,128)}, f32[324,128]{1,0:T(...) custom-call(bf16[512,1152]{1,0:T(8,128)(2,1)} %get-tuple-element.21.refs_0_, bf16[2,1152]{1,0:T(2,128)(2,1)} %get-tuple-element.22.refs_1_, ...), custom_call_target="tpu_custom_call" | custom-call | tf_op jit(solution)/shard_map/pallas_call | solution.py:478
  (1 shorter events, 0.0 us)

commit v4 on v3

--- a/solution.py
+++ b/solution.py
@@ -168,11 +168,12 @@
             preferred_element_type=jnp.float32,
         )
 
-    total = None
-    for i in range(embed_cot.shape[0]):
-        term = freq_now[:, i : i + 1] * embed_cot[i : i + 1, :].astype(jnp.float32)
-        total = term if total is None else total + term
-    grad_e[...] = total
+    grad_e[...] = lax.dot_general(
+        freq_now[...],
+        embed_cot[...],
+        (((0,), (0,)), ((), ())),
+        preferred_element_type=jnp.float32,
+    )
 
     stage[...] = jnp.zeros_like(stage)
     order = [lax.rem(z + 1 + k, nz) for k in range(nz)]
@@ -406,7 +407,7 @@
 def exchange(n, attended, proj_cot, freq_now, embed_cot, attended_next, freq_next, states):
     nz, ny, nx = factor(n)
     width = attended.shape[1]
-    width_e = freq_now.shape[0]
+    width_e = freq_now.shape[1]
     columns = width // LANES
     rows, rows_embed = width // n, width_e // n
     group = max(16 // math.gcd(rows, 16), 16 // math.gcd(rows_embed, 16))
@@ -501,7 +502,7 @@
     width = attended.shape[1]
     freq_width = master_embed.shape[0] * lax.axis_size("dp") // width
     n = lax.axis_size("dp")
-    freq_now = freq_embed(timesteps, freq_width).astype(jnp.float32).T
+    freq_now = freq_embed(timesteps, freq_width)
     freq_next = freq_embed(timesteps_next, freq_width)
     states = (
         master_proj,

time: 67.6 us -> 66.6 us (0.985)
  local copies, waits for them, and re-layouts: 0.8 us -> 0 us
    transpose x1 -> x0, local copies, waits for them, and re-layouts: 0.8 us -> none  [per_device(): freq_now = freq_embed(timesteps, freq_width).astype(jnp.float32).T]
where the time goes in v4:
time: 66.6 us; the launch traced here: 66.4 us
  Pallas kernels  63.8 us (96%)
  other arithmetic  2.02 us (3%)
    pallas_call x1, Pallas kernels, exchange(): pl.pallas_call(functools.partial(exchange_kernel, n, rows, rows_embed), o...  61.2 us
    pallas_call x1, Pallas kernels, exchange(): pl.pallas_call(copy_kernel, out_shape=results, in_specs=[vmem] * 7, out_s...  2.59 us

profile of v4, /device:TPU:1, one launch (start us, length us, event | category | flops | bytes accessed | tf_op | source)
XLA Modules:
  0.0 66.4 jit_solution(6189211784162875073)
XLA Ops:
  0.6 0.7 broadcast_multiply_fusion.1
  1.3 0.7 broadcast_multiply_fusion
  2.0 0.1 fusion.2
  2.1 0.6 pad_maximum_fusion
  2.7 61.2 %shard_map.171 = (bf16[512,1152]{1,0:T(8,128)(2,1)}, bf16[2,1152]{1,0:T(2,128)(2,1)}, f32[324,128]{1,0:T(8,128)}, f32[72,128]{1,0:T(8,128)}, f32[324,128]{1,0:T(...) custom-call(bf16[512,1152]{1,0:T(8,128)(2,1)} %attended.1, bf16[512,1152]{1,0:T(8,128)(2,1)} %proj_cot.1, ...), custom_call_target="tpu_custom_call" | custom-call | tf_op jit(solution)/shard_map/pallas_call | solution.py:434
  63.8 2.6 %shard_map.172 = (bf16[512,1152]{1,0:T(8,128)(2,1)}, bf16[2,1152]{1,0:T(2,128)(2,1)}, f32[324,128]{1,0:T(8,128)}, f32[72,128]{1,0:T(8,128)}, f32[324,128]{1,0:T(...) custom-call(bf16[512,1152]{1,0:T(8,128)(2,1)} %get-tuple-element.21.refs_0_, bf16[2,1152]{1,0:T(2,128)(2,1)} %get-tuple-element.22.refs_1_, ...), custom_call_target="tpu_custom_call" | custom-call | tf_op jit(solution)/shard_map/pallas_call | solution.py:479
  (1 shorter events, 0.0 us)
